TPU v7x, 8 devices: a whole 2x2x1 slice. The times are simulated.
8 devices in a mesh: dp: 1 (over z), col: 2 (over y), row: 4 (over x, core).
Axes of the slice: x: 2, y: 2, z: 1, core: 2. Of those that a mesh axis runs over, the one named last changes fastest.
Arguments:
- x_in: bfloat16 [2048, 2048], P(('dp', 'row'), 'col')
- w_qkv: bfloat16 [2048, 6144], P('row', 'col')
- w_out: bfloat16 [2048, 2048], P('row', 'col')
- doc_ids: int32 [2048], P(('dp', 'row'))
- grad_y: bfloat16 [2048, 2048], P(('dp', 'row'), 'col')
Outputs:
- output 1: bfloat16 [2048, 2048], P(('dp', 'row'), 'col')
- output 2: bfloat16 [2048, 6144], P(('dp', 'row'), 'col')
- output 3: bfloat16 [2048, 2048], P(('dp', 'row'), 'col')
All inputs are finite; a program needn't handle non-finite values.
Results may differ from a plain program's by a relative error of at most 0.00385.
Values are sent between devices in bfloat16 or wider.
A program may use at most 1 GiB of HBM per device.

v0:
```python
import jax
import jax.numpy as jnp
from jax import lax
from jax.experimental import pallas as pl
from jax.experimental.pallas import tpu as pltpu
from jax.sharding import PartitionSpec as P

NT = (((1,), (1,)), ((), ()))
TN = (((0,), (0,)), ((), ()))
BQ = 256
BK = 512
D = 128

def attn_kernel(seg_ref, qkv_ref, do_ref, dqkv_ref, o_ref, cut, s_scr, dp_scr, dk_acc, dv_acc):
    qb = pl.program_id(0)
    n_q = pl.num_programs(0)
    seq = qkv_ref.shape[0]
    heads = qkv_ref.shape[1] // (3 * D)
    scale = D ** -0.5

    @pl.when(qb == 0)
    def _():
        seg = seg_ref[...]
        cut[0] = jnp.sum((seg < 1).astype(jnp.int32))
        cut[1] = jnp.sum((seg < 2).astype(jnp.int32))
        dk_acc[...] = jnp.zeros_like(dk_acc)
        dv_acc[...] = jnp.zeros_like(dv_acc)

    c1 = cut[0]
    c2 = cut[1]
    q0 = qb * BQ
    q1 = q0 + BQ - 1
    lo = jnp.where(q0 >= c2, c2, jnp.where(q0 >= c1, c1, 0))
    hi = jnp.where(q1 < c1, c1, jnp.where(q1 < c2, c2, seq))
    b_lo = lo // BK
    b_hi = (hi + BK - 1) // BK
    rows = pl.ds(pl.multiple_of(q0, BQ), BQ)
    iq = q0 + lax.broadcasted_iota(jnp.int32, (BQ, 1), 0)
    dq_doc = (iq >= c1).astype(jnp.int32) + (iq >= c2).astype(jnp.int32)
    q = [qkv_ref[rows, 3 * D * h:3 * D * h + D] for h in range(heads)]
    do = [do_ref[rows, D * h:D * h + D] for h in range(heads)]

    def first(kb, m):
        k0 = pl.multiple_of(kb * BK, BK)
        keys = pl.ds(k0, BK)
        ik = k0 + lax.broadcasted_iota(jnp.int32, (1, BK), 1)
        k_doc = (ik >= c1).astype(jnp.int32) + (ik >= c2).astype(jnp.int32)
        same = dq_doc == k_doc
        out = []
        for h in range(heads):
            k = qkv_ref[keys, 3 * D * h + D:3 * D * h + 2 * D]
            v = qkv_ref[keys, 3 * D * h + 2 * D:3 * D * h + 3 * D]
            s = lax.dot_general(q[h], k, NT, preferred_element_type=jnp.float32) * scale
            s = jnp.where(same, s, -jnp.inf)
            s_scr[h, :, keys] = s
            dp_scr[h, :, keys] = lax.dot_general(do[h], v, NT, preferred_element_type=jnp.float32)
            out.append(jnp.maximum(m[h], jnp.max(s, axis=1, keepdims=True)))
        return tuple(out)

    m = lax.fori_loop(b_lo, b_hi, first, tuple(jnp.full((BQ, 1), -jnp.inf, jnp.float32) for _ in range(heads)))

    def second(kb, ld):
        keys = pl.ds(pl.multiple_of(kb * BK, BK), BK)
        out = []
        for h in range(heads):
            p = jnp.exp(s_scr[h, :, keys] - m[h])
            s_scr[h, :, keys] = p
            l, dd = ld[h]
            out.append((l + jnp.sum(p, axis=1, keepdims=True), dd + jnp.sum(p * dp_scr[h, :, keys], axis=1, keepdims=True)))
        return tuple(out)

    zero = jnp.zeros((BQ, 1), jnp.float32)
    ld = lax.fori_loop(b_lo, b_hi, second, tuple((zero, zero) for _ in range(heads)))
    inv = [1.0 / ld[h][0] for h in range(heads)]
    row_dot = [ld[h][1] * inv[h] for h in range(heads)]
    inv_sc = [inv[h] * scale for h in range(heads)]

    def third(kb, acc):
        keys = pl.ds(pl.multiple_of(kb * BK, BK), BK)
        out = []
        for h in range(heads):
            k = qkv_ref[keys, 3 * D * h + D:3 * D * h + 2 * D]
            v = qkv_ref[keys, 3 * D * h + 2 * D:3 * D * h + 3 * D]
            p = s_scr[h, :, keys]
            p_bf = (p * inv[h]).astype(jnp.bfloat16)
            ds = ((p * inv_sc[h]) * (dp_scr[h, :, keys] - row_dot[h])).astype(jnp.bfloat16)
            o, dq = acc[h]
            o = o + jnp.dot(p_bf, v, preferred_element_type=jnp.float32)
            dq = dq + jnp.dot(ds, k, preferred_element_type=jnp.float32)
            dk_acc[h, keys, :] += lax.dot_general(ds, q[h], TN, preferred_element_type=jnp.float32)
            dv_acc[h, keys, :] += lax.dot_general(p_bf, do[h], TN, preferred_element_type=jnp.float32)
            out.append((o, dq))
        return tuple(out)

    zacc = jnp.zeros((BQ, D), jnp.float32)
    acc = lax.fori_loop(b_lo, b_hi, third, tuple((zacc, zacc) for _ in range(heads)))
    for h in range(heads):
        o_ref[rows, D * h:D * h + D] = acc[h][0].astype(jnp.bfloat16)
        dqkv_ref[rows, 3 * D * h:3 * D * h + D] = acc[h][1].astype(jnp.bfloat16)

    @pl.when(qb == n_q - 1)
    def _():
        for h in range(heads):
            dqkv_ref[:, 3 * D * h + D:3 * D * h + 2 * D] = dk_acc[h].astype(jnp.bfloat16)
            dqkv_ref[:, 3 * D * h + 2 * D:3 * D * h + 3 * D] = dv_acc[h].astype(jnp.bfloat16)

def attention(seg_row, qkv, d_attn):
    seq, width = qkv.shape
    heads = width // (3 * D)
    full = lambda shape: pl.BlockSpec(shape, lambda i: tuple(0 for _ in shape))
    return pl.pallas_call(
        attn_kernel,
        grid=(seq // BQ,),
        in_specs=[full(seg_row.shape), full(qkv.shape), full(d_attn.shape)],
        out_specs=[full(qkv.shape), full(d_attn.shape)],
        out_shape=[jax.ShapeDtypeStruct(qkv.shape, jnp.bfloat16), jax.ShapeDtypeStruct(d_attn.shape, jnp.bfloat16)],
        scratch_shapes=[
            pltpu.SMEM((2,), jnp.int32),
            pltpu.VMEM((heads, BQ, seq), jnp.float32),
            pltpu.VMEM((heads, BQ, seq), jnp.float32),
            pltpu.VMEM((heads, seq, D), jnp.float32),
            pltpu.VMEM((heads, seq, D), jnp.float32),
        ],
        compiler_params=pltpu.CompilerParams(dimension_semantics=("arbitrary",), vmem_limit_bytes=60 * 1024 * 1024),
    )(seg_row, qkv, d_attn)


MESH = pl.DeviceIdType.MESH
NC = 2


def place():
    y = lax.axis_index('col')
    r = lax.axis_index('row')
    c = lax.rem(r, 2)
    r_s = r + 1 - 2 * c
    return y, r, c, r_s, lax.rem(r + 2, 4), lax.rem(r_s + 2, 4)


def mult(i, n):
    return pl.multiple_of(i * n, n)


def gather_kernel(x_ref, w_ref, wo_ref, seg_ref, dy_ref, xg, dyg, wg, segg, qkv_ref, do_ref,
                  stage, wstage, wh, woh, tok, ssem, rsem, lsem):
    y, r, c, r_s, r_x, r_xs = place()
    x = r // 2
    t_loc, h_loc = x_ref.shape
    hw = wh.shape[1]
    ow = woh.shape[0]
    sib, xn, yn = {'row': r_s}, {'row': r_x}, {'col': 1 - y}
    ct = t_loc // NC
    started = []

    def send(i, src, dst, dev):
        cp = pltpu.make_async_remote_copy(src, dst, ssem.at[i], rsem.at[i], device_id=dev, device_id_type=MESH)
        cp.start()
        started.append(cp)

    def recv(i, dst):
        pltpu.make_async_remote_copy(dst, dst, ssem.at[i], rsem.at[i], device_id=sib, device_id_type=MESH).wait_recv()

    def local(i, src, dst):
        cp = pltpu.make_async_copy(src, dst, lsem.at[i])
        cp.start()
        return cp

    def slot(g, yy, rr, j):
        return g.at[pl.ds(pl.multiple_of(rr * t_loc + j * ct, ct), ct), pl.ds(mult(yy, h_loc), h_loc)]

    def own(a, j):
        return a.at[pl.ds(j * ct, ct)]

    def tid(base, kind, j):
        return base + kind * NC + j

    XB, YB = 0, 7 * NC
    WB = 14 * NC
    WOB = WB + 12
    SGB = WOB + 2

    def got_from(kind):
        return ((y, r_s), (y, r_x), (1 - y, r), (y, r_xs), (1 - y, r_x), (1 - y, r_s), (1 - y, r_xs))[kind]

    def send_own(a, g, base, kind, dev):
        for j in range(NC):
            send(tid(base, kind, j), own(a, j), slot(g, y, r, j), dev)

    def forward(g, base, kind_in, outs, j):
        yy, rr = got_from(kind_in)
        recv(tid(base, kind_in, j), slot(g, yy, rr, j))
        for kind_out, dev in outs:
            send(tid(base, kind_out, j), slot(g, yy, rr, j), slot(g, yy, rr, j), dev)

    def take(g, base, kind):
        yy, rr = got_from(kind)
        for j in range(NC):
            recv(tid(base, kind, j), slot(g, yy, rr, j))

    def wslot(rr, q):
        return wg.at[pl.ds(mult(rr, t_loc), t_loc), pl.ds(mult(q, hw), hw)]

    def wq(t, xx):
        return lax.rem(2 * xx + t, 4)

    def w_own(t, kind, xx, dev):
        q = wq(t, xx)
        send(WB + 4 * kind + t, w_ref.at[:, pl.ds(mult(q, hw), hw)], wslot(r, q), dev)

    def w_forward(t):
        q = wq(t, x)
        recv(WB + 4 + t, wslot(r_x, q))
        send(WB + 8 + t, wslot(r_x, q), wslot(r_x, q), sib)

    for i, (rr, dev) in enumerate(((r_s, sib), (r_x, xn), (r_xs, {'row': r_xs}))):
        send(SGB + i, seg_ref, segg.at[r], dev)
    send_own(x_ref, xg, XB, 1, xn)
    send_own(x_ref, xg, XB, 2, yn)
    for t in range(2):
        w_own(t, 1, 1 - x, xn)
    send_own(x_ref, xg, XB, 0, sib)
    for t in range(4):
        w_own(t, 0, x, sib)
    for k in range(2):
        row_to = 2 * c + k
        src = wo_ref.at[pl.ds(k * ow, ow)]
        dst = woh.at[:, pl.ds(mult(y, h_loc), h_loc)]
        mine = (x == y) & (row_to == r)

        @pl.when(mine)
        def _():
            pltpu.make_async_copy(src, dst, lsem.at[0]).start()

        @pl.when(jnp.logical_not(mine))
        def _():
            pltpu.make_async_remote_copy(src, dst, ssem.at[WOB + k], rsem.at[WOB + y],
                                         device_id={'col': x, 'row': row_to}, device_id_type=MESH).start()
    send_own(dy_ref, dyg, YB, 1, xn)
    send_own(dy_ref, dyg, YB, 0, sib)
    for t in range(2, 4):
        w_own(t, 1, 1 - x, xn)

    a = local(1, x_ref, stage.at[0])
    b = local(2, dy_ref, stage.at[1])
    d = local(3, w_ref, wstage)
    sg = local(4, seg_ref, segg.at[r])
    own_slot = lambda g: g.at[pl.ds(mult(r, t_loc), t_loc), pl.ds(mult(y, h_loc), h_loc)]
    a.wait()
    a = local(1, stage.at[0], own_slot(xg))
    b.wait()
    b = local(2, stage.at[1], own_slot(dyg))
    d.wait()
    d = local(3, wstage, wg.at[pl.ds(mult(r, t_loc), t_loc)])
    wh[pl.ds(mult(r, t_loc), t_loc), :] = wstage[:, pl.ds(mult(r, hw), hw)]

    for j in range(NC):
        forward(xg, XB, 1, ((4, yn), (3, sib)), j)
        forward(xg, XB, 2, ((5, sib),), j)
    send_own(dy_ref, dyg, YB, 2, yn)
    for j in range(NC):
        w_forward(j)
        forward(xg, XB, 4, ((6, sib),), j)
    a.wait()
    b.wait()
    d.wait()
    sg.wait()

    for t in range(4):
        recv(WB + t, wslot(r_s, wq(t, x)))
    for t in range(2):
        recv(WB + 8 + t, wslot(r_xs, wq(t, x)))
    loads = []
    for i, rr in enumerate((r_s, r_x, r_xs)):
        loads.append(local(5 + i, wslot(rr, r), wh.at[pl.ds(mult(rr, t_loc), t_loc)]))
    for kind in (0, 3, 5, 6):
        take(xg, XB, kind)

    def load_tok(g, rr, s):
        return local(8 + s, g.at[pl.ds(mult(rr, t_loc), t_loc)], tok.at[s])

    blocks = (r, r_s, r_x, r_xs)
    nxt = load_tok(xg, blocks[0], 0)
    for cp in loads:
        cp.wait()
    for i in range(4):
        nxt.wait()
        if i < 3:
            nxt = load_tok(xg, blocks[i + 1], (i + 1) % 2)
        rows = pl.ds(mult(blocks[i], t_loc), t_loc)
        for n in range(hw // 256):
            cols = slice(256 * n, 256 * n + 256)
            qkv_ref[rows, cols] = jnp.dot(tok[i % 2], wh[:, cols], preferred_element_type=jnp.float32).astype(jnp.bfloat16)

    for j in range(NC):
        forward(dyg, YB, 1, ((4, yn), (3, sib)), j)
        forward(dyg, YB, 2, ((5, sib),), j)
    for yy in range(2):
        piece = woh.at[:, pl.ds(yy * h_loc, h_loc)]
        mine = (y == yy) & (2 * y + x == r)

        @pl.when(mine)
        def _():
            pltpu.make_async_copy(wo_ref.at[pl.ds(0, ow)], piece, lsem.at[0]).wait()

        @pl.when(jnp.logical_not(mine))
        def _():
            recv(WOB + yy, piece)
    for kind in (0, 5):
        take(dyg, YB, kind)

    def d_out(i, s):
        rows = pl.ds(mult(blocks[i], t_loc), t_loc)
        do_ref[rows, :] = lax.dot_general(tok[s], woh[...], NT, preferred_element_type=jnp.float32).astype(jnp.bfloat16)

    one = load_tok(dyg, r, 0)
    two = load_tok(dyg, r_s, 1)
    one.wait()
    d_out(0, 0)
    two.wait()
    d_out(1, 1)
    for j in range(NC):
        forward(dyg, YB, 4, ((6, sib),), j)
    w_forward(2)
    take(dyg, YB, 3)
    one = load_tok(dyg, r_x, 0)
    take(dyg, YB, 6)
    two = load_tok(dyg, r_xs, 1)
    one.wait()
    d_out(2, 0)
    two.wait()
    d_out(3, 1)
    w_forward(3)
    for t in range(2, 4):
        recv(WB + 8 + t, wslot(r_xs, wq(t, x)))
    for i, rr in enumerate((r_s, r_x, r_xs)):
        recv(SGB + i, segg.at[rr])
    for cp in started:
        cp.wait_send()
    for k in range(2):
        mine = (x == y) & (2 * c + k == r)

        @pl.when(jnp.logical_not(mine))
        def _():
            pltpu.make_async_remote_copy(wo_ref.at[pl.ds(0, ow)], woh.at[:, pl.ds(0, h_loc)], ssem.at[WOB + k], rsem.at[WOB + k],
                                         device_id=sib, device_id_type=MESH).wait_send()


def gather_all(x_blk, w_blk, wo_blk, seg_blk, dy_blk):
    t_loc, h_loc = x_blk.shape
    w_loc = w_blk.shape[1]
    seq, hid = 4 * t_loc, 2 * h_loc
    hw, ow = w_loc // 4, w_loc // 12
    bf = jnp.bfloat16
    hbm = pl.BlockSpec(memory_space=pl.ANY)
    vmem = pl.BlockSpec(memory_space=pltpu.VMEM)
    n_sem = 14 * NC + 12 + 2 + 3
    return pl.pallas_call(
        gather_kernel,
        in_specs=[hbm] * 5,
        out_specs=[hbm] * 4 + [vmem] * 2,
        out_shape=[
            jax.ShapeDtypeStruct((seq, hid), bf), jax.ShapeDtypeStruct((seq, hid), bf),
            jax.ShapeDtypeStruct((hid, w_loc), bf), jax.ShapeDtypeStruct((4,) + seg_blk.shape, jnp.int32),
            jax.ShapeDtypeStruct((seq, hw), bf), jax.ShapeDtypeStruct((seq, ow), bf),
        ],
        scratch_shapes=[
            pltpu.VMEM((2, t_loc, h_loc), bf), pltpu.VMEM((t_loc, w_loc), bf), pltpu.VMEM((hid, hw), bf),
            pltpu.VMEM((ow, hid), bf), pltpu.VMEM((2, t_loc, hid), bf),
            pltpu.SemaphoreType.DMA((n_sem,)), pltpu.SemaphoreType.DMA((n_sem,)), pltpu.SemaphoreType.DMA((10,)),
        ],
        compiler_params=pltpu.CompilerParams(has_side_effects=True, vmem_limit_bytes=48 * 1024 * 1024),
        name='gather_project',
    )(x_blk, w_blk, wo_blk, seg_blk, dy_blk)


NJ = 2


def scatter_kernel(xg, dyg, wg, dqkv_ref, o_ref, dx_out, dw_out, dwo_out,
                   dtok, dq_v, w_v, o_v, col_v, dw_v, dwo_v, px_send, px_recv, px_own, dx_v, ssem, rsem, lsem):
    y, r, c, r_s, r_x, r_xs = place()
    x = r // 2
    t_loc, feat = dtok.shape
    hw = dq_v.shape[1]
    ow = o_v.shape[1]
    seq = dq_v.shape[0]
    h_loc = dx_v.shape[1]
    bt = t_loc // NJ
    f32 = jnp.float32
    others = (r_s, r_x, r_xs)
    started = []
    DQ, DW, DWO, PX = 0, 3 * NJ, 3 * NJ + 3, 3 * NJ + 5

    def copy(i, k, src, dst, dev):
        return pltpu.make_async_remote_copy(src, dst, ssem.at[i], rsem.at[k], device_id=dev, device_id_type=MESH)

    def send(i, src, dst, dev):
        cp = copy(i, i, src, dst, dev)
        cp.start()
        started.append(cp)

    def recv(i, dst):
        copy(i, i, dst, dst, {'row': r_s}).wait_recv()

    def local(i, src, dst):
        cp = pltpu.make_async_copy(src, dst, lsem.at[i])
        cp.start()
        return cp

    def tok_slot(rr, j):
        return dtok.at[pl.ds(j * bt, bt), pl.ds(mult(rr, hw), hw)]

    def dw_slot(rr):
        return dw_out.at[:, pl.ds(mult(rr, hw), hw)]

    for j in range(NJ):
        for k in (1, 2, 0):
            rr = others[k]
            src = dqkv_ref.at[pl.ds(pl.multiple_of(rr * t_loc + j * bt, bt), bt)]
            send(DQ + 3 * j + k, src, tok_slot(r, j), {'row': rr})
    own_tok = local(0, dqkv_ref.at[pl.ds(mult(r, t_loc), t_loc)], dtok.at[:, pl.ds(mult(r, hw), hw)])
    ld_o = local(1, o_ref, o_v)
    ld_dy = [local(2 + s, dyg.at[:, pl.ds(512 * s, 512)], col_v.at[s]) for s in range(2)]
    ld_dq = local(4, dqkv_ref, dq_v)
    ld_w = local(5, wg, w_v)

    ld_o.wait()
    ld_x = [None, None]
    blocks = (r_x, r_xs, r_s, r)
    for s in range(4):
        ld_dy[s].wait()
        dwo_v[:, 512 * s:512 * s + 512] = lax.dot_general(o_v[...], col_v[s % 2], TN, preferred_element_type=f32).astype(jnp.bfloat16)
        if s < 2:
            ld_dy.append(local(2 + s, dyg.at[:, pl.ds(512 * s + 1024, 512)], col_v.at[s]))
        else:
            ld_x[s - 2] = local(2 + s - 2, xg.at[:, pl.ds(mult(blocks[s - 2], t_loc), t_loc)], col_v.at[s - 2])
    row_to = 2 * y + x
    for k in range(2):
        src = dwo_v.at[:, pl.ds(k * h_loc, h_loc)]
        dst = dwo_out.at[pl.ds(mult(c, ow), ow)]
        mine = (y == k) & (row_to == r)

        @pl.when(mine)
        def _():
            pltpu.make_async_copy(src, dst, lsem.at[6]).start()

        @pl.when(jnp.logical_not(mine))
        def _():
            copy(DWO + k, DWO + c, src, dst, {'col': k, 'row': row_to}).start()

    ld_dq.wait()

    def d_w(i):
        s = i % 2
        ld_x[s].wait()
        dw_v[i] = lax.dot_general(col_v[s], dq_v[...], TN, preferred_element_type=f32).astype(jnp.bfloat16)
        if i < 2:
            ld_x[s] = local(2 + s, xg.at[:, pl.ds(mult(blocks[i + 2], t_loc), t_loc)], col_v.at[s])

    def d_x(j, half, dst):
        for n in range(h_loc // 256):
            rows = pl.ds(pl.multiple_of(half * h_loc + 256 * n, 256), 256)
            dst[pl.ds(j * bt, bt), 256 * n:256 * n + 256] = lax.dot_general(
                dtok[pl.ds(j * bt, bt), :], w_v[rows, :], NT, preferred_element_type=f32)

    def d_x_send(j):
        for k in range(3):
            recv(DQ + 3 * j + k, tok_slot(others[k], j))
        d_x(j, 1 - y, px_send)
        send(PX + j, px_send.at[pl.ds(j * bt, bt)], px_recv.at[pl.ds(j * bt, bt)], {'col': 1 - y})

    d_w(0)
    send(DW + 1, dw_v.at[0], dw_slot(r), {'row': r_x})
    d_w(1)
    send(DW + 2, dw_v.at[1], dw_slot(r), {'row': r_xs})
    ld_w.wait()
    own_tok.wait()
    d_x_send(0)
    d_w(2)
    send(DW + 0, dw_v.at[2], dw_slot(r), {'row': r_s})
    d_x(0, y, px_own)
    d_x_send(1)
    d_w(3)
    own_dw = local(0, dw_v.at[3], dw_slot(r))
    d_x(1, y, px_own)
    outs = []
    for j in range(NJ):
        rows = pl.ds(j * bt, bt)
        recv(PX + j, px_recv.at[rows])
        dx_v[rows, :] = (px_own[rows, :] + px_recv[rows, :]).astype(jnp.bfloat16)
        outs.append(local(2 + j, dx_v.at[rows], dx_out.at[rows]))
    own_dw.wait()
    for k in range(3):
        recv(DW + k, dw_slot(others[k]))
    for k in range(2):
        piece = dwo_out.at[pl.ds(k * ow, ow)]
        mine = (r // 2 == y) & (2 * lax.rem(r, 2) + k == r)

        @pl.when(mine)
        def _():
            pltpu.make_async_copy(dwo_v.at[:, pl.ds(0, h_loc)], piece, lsem.at[6]).wait()

        @pl.when(jnp.logical_not(mine))
        def _():
            recv(DWO + k, piece)
    for cp in outs:
        cp.wait()
    for cp in started:
        cp.wait_send()
    for k in range(2):
        @pl.when(jnp.logical_not((y == k) & (row_to == r)))
        def _():
            copy(DWO + k, DWO + k, dwo_v.at[:, pl.ds(0, h_loc)], dwo_out.at[pl.ds(0, ow)], {'row': r_s}).wait_send()


def scatter_all(x_all, dy_all, w_col, d_qkv, attn_out, blocks):
    bf, f32 = jnp.bfloat16, jnp.float32
    t_loc, h_loc = blocks[0].shape
    seq, hw = d_qkv.shape
    ow = attn_out.shape[1]
    hid, feat = w_col.shape
    hbm = pl.BlockSpec(memory_space=pl.ANY)
    n_sem = 4 * NJ + 5
    return pl.pallas_call(
        scatter_kernel,
        in_specs=[hbm] * 5,
        out_specs=[hbm] * 3,
        out_shape=[jax.ShapeDtypeStruct(b.shape, bf) for b in blocks],
        scratch_shapes=[
            pltpu.VMEM((t_loc, feat), bf), pltpu.VMEM((seq, hw), bf), pltpu.VMEM((hid, feat), bf), pltpu.VMEM((seq, ow), bf),
            pltpu.VMEM((2, seq, t_loc), bf), pltpu.VMEM((4, t_loc, hw), bf), pltpu.VMEM((ow, hid), bf),
            pltpu.VMEM((t_loc, h_loc), f32), pltpu.VMEM((t_loc, h_loc), f32), pltpu.VMEM((t_loc, h_loc), f32),
            pltpu.VMEM((t_loc, h_loc), bf),
            pltpu.SemaphoreType.DMA((n_sem,)), pltpu.SemaphoreType.DMA((n_sem,)), pltpu.SemaphoreType.DMA((7,)),
        ],
        compiler_params=pltpu.CompilerParams(has_side_effects=True, vmem_limit_bytes=60 * 1024 * 1024),
        name='project_scatter',
    )(x_all, dy_all, w_col, d_qkv, attn_out)


def solution(mesh):
    tok_spec = P(('dp', 'row'), 'col')
    mat_spec = P('row', 'col')
    seg_spec = P(('dp', 'row'))

    def grad_step(x_blk, wqkv_blk, wout_blk, seg_blk, dy_blk):
        x_all, dy_all, w_col, seg_all, qkv, d_attn = gather_all(x_blk, wqkv_blk, wout_blk, seg_blk.reshape(4, -1), dy_blk)
        d_qkv, attn_out = attention(seg_all, qkv, d_attn)
        grad_x, grad_wqkv, grad_wout = scatter_all(x_all, dy_all, w_col, d_qkv, attn_out, (x_blk, wqkv_blk, wout_blk))
        return grad_x, grad_wqkv, grad_wout

    return jax.shard_map(grad_step, mesh=mesh, in_specs=(tok_spec, mat_spec, mat_spec, seg_spec, tok_spec), out_specs=(tok_spec, tok_spec, tok_spec), check_vma=False)
```

profile of v0, /device:TPU:0, one launch (start us, length us, event | category | flops | bytes accessed | tf_op | source)
XLA Modules:
  0.0 293.8 jit_solution(2541375390085702406)
XLA Ops:
  0.6 0.0 copy-start
  0.6 1.2 copy-done
  1.9 0.0 copy-start.1
  1.9 1.2 copy-done.1
  3.1 0.0 copy-start.2
  3.1 1.2 copy-done.2
  4.3 0.0 copy-start.5
  4.3 0.7 copy-done.5
  5.0 135.4 %gather_project.1 = (bf16[2048,2048]{1,0:T(8,128)(2,1)}, bf16[2048,2048]{1,0:T(8,128)(2,1)}, bf16[2048,3072]{1,0:T(8,128)(2,1)}, s32[4,4,128]{2,1,0:T(4,128)S(1)...) custom-call(bf16[512,1024]{1,0:T(8,128)(2,1)S(1)} %copy-done, bf16[512,3072]{1,0:T(8,128)(2,1)} %w_ref.1, ...), custom_call_target="tpu_custom_call" | custom-call | tf_op jit(solution)/shard_map/gather_project/pallas_call | solution.py:357
  140.4 0.0 copy-start.3
  140.4 1.0 copy-done.3
  141.4 0.0 copy-start.4
  141.4 0.6 copy-done.4
  142.0 50.6 %shard_map.76 = (bf16[2048,768]{1,0:T(8,128)(2,1)}, bf16[2048,256]{1,0:T(8,128)(2,1)}) custom-call(s32[4,4,128]{2,1,0:T(4,128)} %copy-done.4, bf16[2048,768]{1,0:T(8,128)(2,1)} %get-tuple-element.15.qkv_ref, bf16[2048,256]{1,0:T(8,128)(2,1)} %copy-done.3), custom_call_target="tpu_custom_call" | custom-call | tf_op jit(solution)/shard_map/pallas_call | solution.py:111
  192.6 94.1 %project_scatter.1 = (bf16[512,1024]{1,0:T(8,128)(2,1)}, bf16[512,3072]{1,0:T(8,128)(2,1)}, bf16[512,1024]{1,0:T(8,128)(2,1)}) custom-call(bf16[2048,2048]{1,0:T(8,128)(2,1)} %get-tuple-element.11.xg, bf16[2048,2048]{1,0:T(8,128)(2,1)} %get-tuple-element.12.dyg, bf16[2048,3072]{1,0:T(8,128)(2,1)} %get-tuple-element.13.wg, ...), custom_call_target="tpu_custom_call" | custom-call | tf_op jit(solution)/shard_map/project_scatter/pallas_call | solution.py:524
  286.7 2.3 copy.11
  289.0 0.0 copy-start.6
  289.0 3.8 %copy.12 = bf16[512,3072]{1,0:T(8,128)(2,1)} copy(bf16[512,3072]{1,0:T(8,128)(2,1)} %get-tuple-element.23) | data formatting | bytes 6291456
  292.8 0.0 copy-done.6
  292.8 1.0 copy.13
Async XLA Ops:
  0.6 1.2 copy-start
  1.9 1.2 copy-start.1
  3.1 1.2 copy-start.2
  4.3 0.7 copy-start.5
  140.4 1.0 copy-start.3
  141.4 0.6 copy-start.4
  289.0 3.8 %copy-start.6 = (bf16[512,1024]{1,0:T(8,128)(2,1)S(1)}, bf16[512,1024]{1,0:T(8,128)(2,1)}, u32[]{:S(2)}) copy-start(bf16[512,1024]{1,0:T(8,128)(2,1)} %get-tuple-element.24) | copy-start | bytes 3145732
where the time goes:
time: 297 us; the launch traced here: 294 us
  Pallas kernels  280 us (94%)
  local copies, waits for them, and re-layouts  13 us (4%)
    pallas_call x1, Pallas kernels, gather_all(): pl.pallas_call(gather_kernel, in_specs=[hbm] * 5, out_specs=[hbm] * 4 + [...  135 us
    pallas_call x1, Pallas kernels, scatter_all(): pl.pallas_call(scatter_kernel, in_specs=[hbm] * 5, out_specs=[hbm] * 3, o...  94.1 us
    pallas_call x1, Pallas kernels, attention(): pl.pallas_call(attn_kernel, grid=(seq // BQ,), in_specs=[full(seg_row.sha...  50.6 us
    unnamed x17, local copies, waits for them, and re-layouts  13 us

commit v1 on v0

--- a/solution.py
+++ b/solution.py
@@ -7,122 +7,74 @@
 
 NT = (((1,), (1,)), ((), ()))
 TN = (((0,), (0,)), ((), ()))
-BQ = 256
 BK = 512
 D = 128
-
-def attn_kernel(seg_ref, qkv_ref, do_ref, dqkv_ref, o_ref, cut, s_scr, dp_scr, dk_acc, dv_acc):
-    qb = pl.program_id(0)
-    n_q = pl.num_programs(0)
-    seq = qkv_ref.shape[0]
-    heads = qkv_ref.shape[1] // (3 * D)
+LOW = -3.0e38
+VMEM_LIMIT = 66_000_000
+
+
+def attention_block(q0, bq, c1, c2, qkv_v, do_v, p_scr, dp_scr, m_scr, kt, vt, dk_acc, dv_acc, dqkv_v, o_v):
+    seq = qkv_v.shape[0]
+    heads = do_v.shape[1] // D
     scale = D ** -0.5
-
-    @pl.when(qb == 0)
-    def _():
-        seg = seg_ref[...]
-        cut[0] = jnp.sum((seg < 1).astype(jnp.int32))
-        cut[1] = jnp.sum((seg < 2).astype(jnp.int32))
-        dk_acc[...] = jnp.zeros_like(dk_acc)
-        dv_acc[...] = jnp.zeros_like(dv_acc)
-
-    c1 = cut[0]
-    c2 = cut[1]
-    q0 = qb * BQ
-    q1 = q0 + BQ - 1
-    lo = jnp.where(q0 >= c2, c2, jnp.where(q0 >= c1, c1, 0))
-    hi = jnp.where(q1 < c1, c1, jnp.where(q1 < c2, c2, seq))
-    b_lo = lo // BK
-    b_hi = (hi + BK - 1) // BK
-    rows = pl.ds(pl.multiple_of(q0, BQ), BQ)
-    iq = q0 + lax.broadcasted_iota(jnp.int32, (BQ, 1), 0)
-    dq_doc = (iq >= c1).astype(jnp.int32) + (iq >= c2).astype(jnp.int32)
-    q = [qkv_ref[rows, 3 * D * h:3 * D * h + D] for h in range(heads)]
-    do = [do_ref[rows, D * h:D * h + D] for h in range(heads)]
-
-    def first(kb, m):
+    to_exp2 = scale * 1.4426950408889634
+    f32 = jnp.float32
+    rows = pl.ds(q0, bq)
+    iq = q0 + lax.broadcasted_iota(jnp.int32, (1, bq), 1)
+    q_doc = (iq >= c1).astype(jnp.int32) + (iq >= c2).astype(jnp.int32)
+    q = [qkv_v[rows, 3 * D * h:3 * D * h + D] for h in range(heads)]
+    do = [do_v[rows, D * h:D * h + D] for h in range(heads)]
+
+    def first(kb, carry):
         k0 = pl.multiple_of(kb * BK, BK)
         keys = pl.ds(k0, BK)
-        ik = k0 + lax.broadcasted_iota(jnp.int32, (1, BK), 1)
+        ik = k0 + lax.broadcasted_iota(jnp.int32, (BK, 1), 0)
         k_doc = (ik >= c1).astype(jnp.int32) + (ik >= c2).astype(jnp.int32)
-        same = dq_doc == k_doc
+        same = q_doc == k_doc
         out = []
         for h in range(heads):
-            k = qkv_ref[keys, 3 * D * h + D:3 * D * h + 2 * D]
-            v = qkv_ref[keys, 3 * D * h + 2 * D:3 * D * h + 3 * D]
-            s = lax.dot_general(q[h], k, NT, preferred_element_type=jnp.float32) * scale
-            s = jnp.where(same, s, -jnp.inf)
-            s_scr[h, :, keys] = s
-            dp_scr[h, :, keys] = lax.dot_general(do[h], v, NT, preferred_element_type=jnp.float32)
-            out.append(jnp.maximum(m[h], jnp.max(s, axis=1, keepdims=True)))
+            m, l, dd = carry[h]
+            k = qkv_v[keys, 3 * D * h + D:3 * D * h + 2 * D]
+            v = qkv_v[keys, 3 * D * h + 2 * D:3 * D * h + 3 * D]
+            s = lax.dot_general(k, q[h], NT, preferred_element_type=f32)
+            s = jnp.where(same, s, LOW)
+            dp = lax.dot_general(v, do[h], NT, preferred_element_type=f32)
+            dp_scr[h, keys, :] = dp
+            m_new = jnp.maximum(m, jnp.max(s, axis=0, keepdims=True))
+            p = jnp.exp2((s - m_new) * to_exp2)
+            p_scr[h, keys, :] = p
+            m_scr[kb, h] = m_new
+            alpha = jnp.exp2((m - m_new) * to_exp2)
+            out.append((m_new, alpha * l + jnp.sum(p, axis=0, keepdims=True), alpha * dd + jnp.sum(p * dp, axis=0, keepdims=True)))
         return tuple(out)
 
-    m = lax.fori_loop(b_lo, b_hi, first, tuple(jnp.full((BQ, 1), -jnp.inf, jnp.float32) for _ in range(heads)))
-
-    def second(kb, ld):
+    zero = jnp.zeros((1, bq), f32)
+    low = jnp.full((1, bq), LOW, f32)
+    mld = lax.fori_loop(0, seq // BK, first, tuple((low, zero, zero) for _ in range(heads)))
+    inv = [1.0 / mld[h][1] for h in range(heads)]
+    row_dot = [mld[h][2] * inv[h] for h in range(heads)]
+
+    def second(kb, acc):
         keys = pl.ds(pl.multiple_of(kb * BK, BK), BK)
         out = []
         for h in range(heads):
-            p = jnp.exp(s_scr[h, :, keys] - m[h])
-            s_scr[h, :, keys] = p
-            l, dd = ld[h]
-            out.append((l + jnp.sum(p, axis=1, keepdims=True), dd + jnp.sum(p * dp_scr[h, :, keys], axis=1, keepdims=True)))
-        return tuple(out)
-
-    zero = jnp.zeros((BQ, 1), jnp.float32)
-    ld = lax.fori_loop(b_lo, b_hi, second, tuple((zero, zero) for _ in range(heads)))
-    inv = [1.0 / ld[h][0] for h in range(heads)]
-    row_dot = [ld[h][1] * inv[h] for h in range(heads)]
-    inv_sc = [inv[h] * scale for h in range(heads)]
-
-    def third(kb, acc):
-        keys = pl.ds(pl.multiple_of(kb * BK, BK), BK)
-        out = []
-        for h in range(heads):
-            k = qkv_ref[keys, 3 * D * h + D:3 * D * h + 2 * D]
-            v = qkv_ref[keys, 3 * D * h + 2 * D:3 * D * h + 3 * D]
-            p = s_scr[h, :, keys]
-            p_bf = (p * inv[h]).astype(jnp.bfloat16)
-            ds = ((p * inv_sc[h]) * (dp_scr[h, :, keys] - row_dot[h])).astype(jnp.bfloat16)
+            f = jnp.exp2((m_scr[kb, h] - mld[h][0]) * to_exp2) * inv[h]
+            p = p_scr[h, keys, :]
+            p_bf = (p * f).astype(jnp.bfloat16)
+            ds = ((p * (f * scale)) * (dp_scr[h, keys, :] - row_dot[h])).astype(jnp.bfloat16)
             o, dq = acc[h]
-            o = o + jnp.dot(p_bf, v, preferred_element_type=jnp.float32)
-            dq = dq + jnp.dot(ds, k, preferred_element_type=jnp.float32)
-            dk_acc[h, keys, :] += lax.dot_general(ds, q[h], TN, preferred_element_type=jnp.float32)
-            dv_acc[h, keys, :] += lax.dot_general(p_bf, do[h], TN, preferred_element_type=jnp.float32)
+            o = o + jnp.dot(vt[h, :, keys], p_bf, preferred_element_type=f32)
+            dq = dq + jnp.dot(kt[h, :, keys], ds, preferred_element_type=f32)
+            dk_acc[h, keys, :] += jnp.dot(ds, q[h], preferred_element_type=f32)
+            dv_acc[h, keys, :] += jnp.dot(p_bf, do[h], preferred_element_type=f32)
             out.append((o, dq))
         return tuple(out)
 
-    zacc = jnp.zeros((BQ, D), jnp.float32)
-    acc = lax.fori_loop(b_lo, b_hi, third, tuple((zacc, zacc) for _ in range(heads)))
+    zacc = jnp.zeros((D, bq), f32)
+    acc = lax.fori_loop(0, seq // BK, second, tuple((zacc, zacc) for _ in range(heads)))
     for h in range(heads):
-        o_ref[rows, D * h:D * h + D] = acc[h][0].astype(jnp.bfloat16)
-        dqkv_ref[rows, 3 * D * h:3 * D * h + D] = acc[h][1].astype(jnp.bfloat16)
-
-    @pl.when(qb == n_q - 1)
-    def _():
-        for h in range(heads):
-            dqkv_ref[:, 3 * D * h + D:3 * D * h + 2 * D] = dk_acc[h].astype(jnp.bfloat16)
-            dqkv_ref[:, 3 * D * h + 2 * D:3 * D * h + 3 * D] = dv_acc[h].astype(jnp.bfloat16)
-
-def attention(seg_row, qkv, d_attn):
-    seq, width = qkv.shape
-    heads = width // (3 * D)
-    full = lambda shape: pl.BlockSpec(shape, lambda i: tuple(0 for _ in shape))
-    return pl.pallas_call(
-        attn_kernel,
-        grid=(seq // BQ,),
-        in_specs=[full(seg_row.shape), full(qkv.shape), full(d_attn.shape)],
-        out_specs=[full(qkv.shape), full(d_attn.shape)],
-        out_shape=[jax.ShapeDtypeStruct(qkv.shape, jnp.bfloat16), jax.ShapeDtypeStruct(d_attn.shape, jnp.bfloat16)],
-        scratch_shapes=[
-            pltpu.SMEM((2,), jnp.int32),
-            pltpu.VMEM((heads, BQ, seq), jnp.float32),
-            pltpu.VMEM((heads, BQ, seq), jnp.float32),
-            pltpu.VMEM((heads, seq, D), jnp.float32),
-            pltpu.VMEM((heads, seq, D), jnp.float32),
-        ],
-        compiler_params=pltpu.CompilerParams(dimension_semantics=("arbitrary",), vmem_limit_bytes=60 * 1024 * 1024),
-    )(seg_row, qkv, d_attn)
+        o_v[rows, D * h:D * h + D] = acc[h][0].T.astype(jnp.bfloat16)
+        dqkv_v[rows, 3 * D * h:3 * D * h + D] = acc[h][1].T.astype(jnp.bfloat16)
 
 
 MESH = pl.DeviceIdType.MESH
@@ -141,11 +93,13 @@
     return pl.multiple_of(i * n, n)
 
 
-def gather_kernel(x_ref, w_ref, wo_ref, seg_ref, dy_ref, xg, dyg, wg, segg, qkv_ref, do_ref,
-                  stage, wstage, wh, woh, tok, ssem, rsem, lsem):
+def forward_kernel(x_ref, w_ref, wo_ref, seg_ref, dy_ref, xg, dyg, wg, segg, dqkv_ref, o_ref,
+                   stage, wstage, wh, woh, tok, qkv_v, do_v, seg_v, p_scr, dp_scr, m_scr, kt, vt, dk_acc, dv_acc, dqkv_v, o_v,
+                   ssem, rsem, lsem):
     y, r, c, r_s, r_x, r_xs = place()
     x = r // 2
     t_loc, h_loc = x_ref.shape
+    heads = woh.shape[0] // D
     hw = wh.shape[1]
     ow = woh.shape[0]
     sib, xn, yn = {'row': r_s}, {'row': r_x}, {'col': 1 - y}
@@ -289,7 +243,19 @@
         rows = pl.ds(mult(blocks[i], t_loc), t_loc)
         for n in range(hw // 256):
             cols = slice(256 * n, 256 * n + 256)
-            qkv_ref[rows, cols] = jnp.dot(tok[i % 2], wh[:, cols], preferred_element_type=jnp.float32).astype(jnp.bfloat16)
+            qkv_v[rows, cols] = jnp.dot(tok[i % 2], wh[:, cols], preferred_element_type=jnp.float32).astype(jnp.bfloat16)
+
+        for h in range(heads):
+            kt[h, :, rows] = qkv_v[rows, 3 * D * h + D:3 * D * h + 2 * D].T
+            vt[h, :, rows] = qkv_v[rows, 3 * D * h + 2 * D:3 * D * h + 3 * D].T
+
+    for i, rr in enumerate((r_s, r_x, r_xs)):
+        recv(SGB + i, segg.at[rr])
+    local(4, segg, seg_v).wait()
+    c1 = jnp.sum((seg_v[...] < 1).astype(jnp.int32))
+    c2 = jnp.sum((seg_v[...] < 2).astype(jnp.int32))
+    dk_acc[...] = jnp.zeros_like(dk_acc)
+    dv_acc[...] = jnp.zeros_like(dv_acc)
 
     for j in range(NC):
         forward(dyg, YB, 1, ((4, yn), (3, sib)), j)
@@ -310,16 +276,22 @@
 
     def d_out(i, s):
         rows = pl.ds(mult(blocks[i], t_loc), t_loc)
-        do_ref[rows, :] = lax.dot_general(tok[s], woh[...], NT, preferred_element_type=jnp.float32).astype(jnp.bfloat16)
+        do_v[rows, :] = lax.dot_general(tok[s], woh[...], NT, preferred_element_type=jnp.float32).astype(jnp.bfloat16)
+
+    def attend(i):
+        q0 = mult(blocks[i], t_loc)
+        attention_block(q0, t_loc, c1, c2, qkv_v, do_v, p_scr, dp_scr, m_scr, kt, vt, dk_acc, dv_acc, dqkv_v, o_v)
 
     one = load_tok(dyg, r, 0)
     two = load_tok(dyg, r_s, 1)
     one.wait()
     d_out(0, 0)
+    attend(0)
+    for j in range(NC):
+        forward(dyg, YB, 4, ((6, sib),), j)
     two.wait()
     d_out(1, 1)
-    for j in range(NC):
-        forward(dyg, YB, 4, ((6, sib),), j)
+    attend(1)
     w_forward(2)
     take(dyg, YB, 3)
     one = load_tok(dyg, r_x, 0)
@@ -327,13 +299,20 @@
     two = load_tok(dyg, r_xs, 1)
     one.wait()
     d_out(2, 0)
+    attend(2)
     two.wait()
     d_out(3, 1)
+    attend(3)
     w_forward(3)
     for t in range(2, 4):
         recv(WB + 8 + t, wslot(r_xs, wq(t, x)))
-    for i, rr in enumerate((r_s, r_x, r_xs)):
-        recv(SGB + i, segg.at[rr])
+    for h in range(heads):
+        dqkv_v[:, 3 * D * h + D:3 * D * h + 2 * D] = dk_acc[h].astype(jnp.bfloat16)
+        dqkv_v[:, 3 * D * h + 2 * D:3 * D * h + 3 * D] = dv_acc[h].astype(jnp.bfloat16)
+    out_a = local(0, dqkv_v, dqkv_ref)
+    out_b = local(1, o_v, o_ref)
+    out_a.wait()
+    out_b.wait()
     for cp in started:
         cp.wait_send()
     for k in range(2):
@@ -345,31 +324,38 @@
                                          device_id=sib, device_id_type=MESH).wait_send()
 
 
-def gather_all(x_blk, w_blk, wo_blk, seg_blk, dy_blk):
+def forward_all(x_blk, w_blk, wo_blk, seg_blk, dy_blk):
     t_loc, h_loc = x_blk.shape
     w_loc = w_blk.shape[1]
     seq, hid = 4 * t_loc, 2 * h_loc
     hw, ow = w_loc // 4, w_loc // 12
-    bf = jnp.bfloat16
+    heads = ow // D
+    bf, f32 = jnp.bfloat16, jnp.float32
     hbm = pl.BlockSpec(memory_space=pl.ANY)
-    vmem = pl.BlockSpec(memory_space=pltpu.VMEM)
     n_sem = 14 * NC + 12 + 2 + 3
+    seg_shape = (4,) + seg_blk.shape
     return pl.pallas_call(
-        gather_kernel,
+        forward_kernel,
         in_specs=[hbm] * 5,
-        out_specs=[hbm] * 4 + [vmem] * 2,
+        out_specs=[hbm] * 6,
         out_shape=[
             jax.ShapeDtypeStruct((seq, hid), bf), jax.ShapeDtypeStruct((seq, hid), bf),
-            jax.ShapeDtypeStruct((hid, w_loc), bf), jax.ShapeDtypeStruct((4,) + seg_blk.shape, jnp.int32),
+            jax.ShapeDtypeStruct((hid, w_loc), bf), jax.ShapeDtypeStruct(seg_shape, jnp.int32),
             jax.ShapeDtypeStruct((seq, hw), bf), jax.ShapeDtypeStruct((seq, ow), bf),
         ],
         scratch_shapes=[
             pltpu.VMEM((2, t_loc, h_loc), bf), pltpu.VMEM((t_loc, w_loc), bf), pltpu.VMEM((hid, hw), bf),
             pltpu.VMEM((ow, hid), bf), pltpu.VMEM((2, t_loc, hid), bf),
+            pltpu.VMEM((seq, hw), bf), pltpu.VMEM((seq, ow), bf), pltpu.VMEM(seg_shape, jnp.int32),
+            pltpu.VMEM((heads, seq, t_loc), f32), pltpu.VMEM((heads, seq, t_loc), f32),
+            pltpu.VMEM((seq // BK, heads, 1, t_loc), f32),
+            pltpu.VMEM((heads, D, seq), bf), pltpu.VMEM((heads, D, seq), bf),
+            pltpu.VMEM((heads, seq, D), f32), pltpu.VMEM((heads, seq, D), f32),
+            pltpu.VMEM((seq, hw), bf), pltpu.VMEM((seq, ow), bf),
             pltpu.SemaphoreType.DMA((n_sem,)), pltpu.SemaphoreType.DMA((n_sem,)), pltpu.SemaphoreType.DMA((10,)),
         ],
-        compiler_params=pltpu.CompilerParams(has_side_effects=True, vmem_limit_bytes=48 * 1024 * 1024),
-        name='gather_project',
+        compiler_params=pltpu.CompilerParams(has_side_effects=True, vmem_limit_bytes=VMEM_LIMIT),
+        name='gather_attend',
     )(x_blk, w_blk, wo_blk, seg_blk, dy_blk)
 
 
@@ -533,7 +519,7 @@
             pltpu.VMEM((t_loc, h_loc), bf),
             pltpu.SemaphoreType.DMA((n_sem,)), pltpu.SemaphoreType.DMA((n_sem,)), pltpu.SemaphoreType.DMA((7,)),
         ],
-        compiler_params=pltpu.CompilerParams(has_side_effects=True, vmem_limit_bytes=60 * 1024 * 1024),
+        compiler_params=pltpu.CompilerParams(has_side_effects=True, vmem_limit_bytes=VMEM_LIMIT),
         name='project_scatter',
     )(x_all, dy_all, w_col, d_qkv, attn_out)
 
@@ -544,8 +530,7 @@
     seg_spec = P(('dp', 'row'))
 
     def grad_step(x_blk, wqkv_blk, wout_blk, seg_blk, dy_blk):
-        x_all, dy_all, w_col, seg_all, qkv, d_attn = gather_all(x_blk, wqkv_blk, wout_blk, seg_blk.reshape(4, -1), dy_blk)
-        d_qkv, attn_out = attention(seg_all, qkv, d_attn)
+        x_all, dy_all, w_col, _, d_qkv, attn_out = forward_all(x_blk, wqkv_blk, wout_blk, seg_blk.reshape(4, -1), dy_blk)
         grad_x, grad_wqkv, grad_wout = scatter_all(x_all, dy_all, w_col, d_qkv, attn_out, (x_blk, wqkv_blk, wout_blk))
         return grad_x, grad_wqkv, grad_wout
 

time: 297 us -> 265 us (0.89)
  Pallas kernels: 280 us -> 257 us
  local copies, waits for them, and re-layouts: 13 us -> 7.08 us
    pallas_call x2 -> x1, Pallas kernels: 186 us -> 163 us  [forward_all(): pl.pallas_call(forward_kernel, in_specs=[hbm] * 5, out_specs=[hbm] * 6, o...]
    unnamed x17 -> x5, local copies, waits for them, and re-layouts: 13 us -> 7.08 us
where the time goes in v1:
time: 265 us
  Pallas kernels  257 us (97%)
  local copies, waits for them, and re-layouts  7.08 us (3%)
    pallas_call x1, Pallas kernels, forward_all(): pl.pallas_call(forward_kernel, in_specs=[hbm] * 5, out_specs=[hbm] * 6, o...  163 us
    pallas_call x1, Pallas kernels, scatter_all(): pl.pallas_call(scatter_kernel, in_specs=[hbm] * 5, out_specs=[hbm] * 3, o...  94.1 us
    unnamed x5, local copies, waits for them, and re-layouts  7.08 us

profile of v1, /device:TPU:0, one launch (start us, length us, event | category | flops | bytes accessed | tf_op | source)
XLA Modules:
  0.0 264.6 jit_solution(16949483235714746111)
XLA Ops:
  0.6 162.7 %gather_attend.1 = (bf16[2048,2048]{1,0:T(8,128)(2,1)}, bf16[2048,2048]{1,0:T(8,128)(2,1)}, bf16[2048,3072]{1,0:T(8,128)(2,1)}, s32[4,4,128]{2,1,0:T(4,128)}, bf...) custom-call(bf16[512,1024]{1,0:T(8,128)(2,1)} %x_ref.1, bf16[512,3072]{1,0:T(8,128)(2,1)} %w_ref.1, ...), custom_call_target="tpu_custom_call" | custom-call | tf_op jit(solution)/shard_map/gather_attend/pallas_call | solution.py:337
  163.4 94.1 %project_scatter.1 = (bf16[512,1024]{1,0:T(8,128)(2,1)}, bf16[512,3072]{1,0:T(8,128)(2,1)}, bf16[512,1024]{1,0:T(8,128)(2,1)}) custom-call(bf16[2048,2048]{1,0:T(8,128)(2,1)} %get-tuple-element.8.xg, bf16[2048,2048]{1,0:T(8,128)(2,1)} %get-tuple-element.9.dyg, bf16[2048,3072]{1,0:T(8,128)(2,1)} %get-tuple-element.10.wg, ...), custom_call_target="tpu_custom_call" | custom-call | tf_op jit(solution)/shard_map/project_scatter/pallas_call | solution.py:510
  257.5 2.3 copy.11
  259.8 0.0 copy-start
  259.8 3.8 %copy.12 = bf16[512,3072]{1,0:T(8,128)(2,1)} copy(bf16[512,3072]{1,0:T(8,128)(2,1)} %get-tuple-element.17) | data formatting | bytes 6291456
  263.6 0.0 copy-done
  263.6 1.0 copy.13
Async XLA Ops:
  259.8 3.8 %copy-start = (bf16[512,1024]{1,0:T(8,128)(2,1)S(1)}, bf16[512,1024]{1,0:T(8,128)(2,1)}, u32[]{:S(2)}) copy-start(bf16[512,1024]{1,0:T(8,128)(2,1)} %get-tuple-element.18) | copy-start | bytes 3145732

commit v2 on v1

--- a/solution.py
+++ b/solution.py
@@ -13,7 +13,7 @@
 VMEM_LIMIT = 66_000_000
 
 
-def attention_block(q0, bq, c1, c2, qkv_v, do_v, p_scr, dp_scr, m_scr, kt, vt, dk_acc, dv_acc, dqkv_v, o_v):
+def attention_block(q0, bq, c1, c2, qkv_v, do_v, p_scr, dp_scr, m_scr, kt, vt, dk_acc, dv_acc, dqkv_v, o_v, between=None):
     seq = qkv_v.shape[0]
     heads = do_v.shape[1] // D
     scale = D ** -0.5
@@ -51,6 +51,8 @@
     zero = jnp.zeros((1, bq), f32)
     low = jnp.full((1, bq), LOW, f32)
     mld = lax.fori_loop(0, seq // BK, first, tuple((low, zero, zero) for _ in range(heads)))
+    if between is not None:
+        between()
     inv = [1.0 / mld[h][1] for h in range(heads)]
     row_dot = [mld[h][2] * inv[h] for h in range(heads)]
 
@@ -175,25 +177,6 @@
     send_own(x_ref, xg, XB, 0, sib)
     for t in range(4):
         w_own(t, 0, x, sib)
-    for k in range(2):
-        row_to = 2 * c + k
-        src = wo_ref.at[pl.ds(k * ow, ow)]
-        dst = woh.at[:, pl.ds(mult(y, h_loc), h_loc)]
-        mine = (x == y) & (row_to == r)
-
-        @pl.when(mine)
-        def _():
-            pltpu.make_async_copy(src, dst, lsem.at[0]).start()
-
-        @pl.when(jnp.logical_not(mine))
-        def _():
-            pltpu.make_async_remote_copy(src, dst, ssem.at[WOB + k], rsem.at[WOB + y],
-                                         device_id={'col': x, 'row': row_to}, device_id_type=MESH).start()
-    send_own(dy_ref, dyg, YB, 1, xn)
-    send_own(dy_ref, dyg, YB, 0, sib)
-    for t in range(2, 4):
-        w_own(t, 1, 1 - x, xn)
-
     a = local(1, x_ref, stage.at[0])
     b = local(2, dy_ref, stage.at[1])
     d = local(3, w_ref, wstage)
@@ -210,10 +193,27 @@
     for j in range(NC):
         forward(xg, XB, 1, ((4, yn), (3, sib)), j)
         forward(xg, XB, 2, ((5, sib),), j)
+    for k in range(2):
+        row_to = 2 * c + k
+        src = wo_ref.at[pl.ds(k * ow, ow)]
+        dst = woh.at[:, pl.ds(mult(y, h_loc), h_loc)]
+        mine = (x == y) & (row_to == r)
+
+        @pl.when(mine)
+        def _():
+            pltpu.make_async_copy(src, dst, lsem.at[0]).start()
+
+        @pl.when(jnp.logical_not(mine))
+        def _():
+            pltpu.make_async_remote_copy(src, dst, ssem.at[WOB + k], rsem.at[WOB + y],
+                                         device_id={'col': x, 'row': row_to}, device_id_type=MESH).start()
     send_own(dy_ref, dyg, YB, 2, yn)
-    for j in range(NC):
-        w_forward(j)
-        forward(xg, XB, 4, ((6, sib),), j)
+    send_own(dy_ref, dyg, YB, 1, xn)
+    send_own(dy_ref, dyg, YB, 0, sib)
+    w_forward(0)
+    forward(xg, XB, 4, ((6, sib),), 0)
+    forward(xg, XB, 4, ((6, sib),), 1)
+    w_forward(1)
     a.wait()
     b.wait()
     d.wait()
@@ -258,7 +258,6 @@
     dv_acc[...] = jnp.zeros_like(dv_acc)
 
     for j in range(NC):
-        forward(dyg, YB, 1, ((4, yn), (3, sib)), j)
         forward(dyg, YB, 2, ((5, sib),), j)
     for yy in range(2):
         piece = woh.at[:, pl.ds(yy * h_loc, h_loc)]
@@ -271,36 +270,41 @@
         @pl.when(jnp.logical_not(mine))
         def _():
             recv(WOB + yy, piece)
-    for kind in (0, 5):
-        take(dyg, YB, kind)
 
     def d_out(i, s):
         rows = pl.ds(mult(blocks[i], t_loc), t_loc)
         do_v[rows, :] = lax.dot_general(tok[s], woh[...], NT, preferred_element_type=jnp.float32).astype(jnp.bfloat16)
 
-    def attend(i):
+    def attend(i, between=None):
         q0 = mult(blocks[i], t_loc)
-        attention_block(q0, t_loc, c1, c2, qkv_v, do_v, p_scr, dp_scr, m_scr, kt, vt, dk_acc, dv_acc, dqkv_v, o_v)
-
-    one = load_tok(dyg, r, 0)
-    two = load_tok(dyg, r_s, 1)
-    one.wait()
+        attention_block(q0, t_loc, c1, c2, qkv_v, do_v, p_scr, dp_scr, m_scr, kt, vt, dk_acc, dv_acc, dqkv_v, o_v, between)
+
+    def dy_forward(j):
+        forward(dyg, YB, 1, ((4, yn), (3, sib)), j)
+
+    def w_rest():
+        for t in range(2, 4):
+            w_own(t, 1, 1 - x, xn)
+
+    load_tok(dyg, r, 0).wait()
     d_out(0, 0)
-    attend(0)
-    for j in range(NC):
-        forward(dyg, YB, 4, ((6, sib),), j)
-    two.wait()
+    attend(0, lambda: dy_forward(0))
+    dy_forward(1)
+    w_rest()
+    for kind in (0, 5):
+        take(dyg, YB, kind)
+    load_tok(dyg, r_s, 1).wait()
     d_out(1, 1)
-    attend(1)
-    w_forward(2)
-    take(dyg, YB, 3)
+    attend(1, lambda: forward(dyg, YB, 4, ((6, sib),), 0))
+    forward(dyg, YB, 4, ((6, sib),), 1)
     one = load_tok(dyg, r_x, 0)
-    take(dyg, YB, 6)
-    two = load_tok(dyg, r_xs, 1)
     one.wait()
     d_out(2, 0)
+    take(dyg, YB, 3)
     attend(2)
-    two.wait()
+    w_forward(2)
+    take(dyg, YB, 6)
+    load_tok(dyg, r_xs, 1).wait()
     d_out(3, 1)
     attend(3)
     w_forward(3)
@@ -363,7 +367,7 @@
 
 
 def scatter_kernel(xg, dyg, wg, dqkv_ref, o_ref, dx_out, dw_out, dwo_out,
-                   dtok, dq_v, w_v, o_v, col_v, dw_v, dwo_v, px_send, px_recv, px_own, dx_v, ssem, rsem, lsem):
+                   dtok, dq_v, w_v, o_v, col_v, dw_v, dwo_v, px_send, px_recv, px_own, dx_v, relay, ssem, rsem, lsem):
     y, r, c, r_s, r_x, r_xs = place()
     x = r // 2
     t_loc, feat = dtok.shape
@@ -376,6 +380,8 @@
     others = (r_s, r_x, r_xs)
     started = []
     DQ, DW, DWO, PX = 0, 3 * NJ, 3 * NJ + 3, 3 * NJ + 5
+    DWF = PX + NJ
+    DWG = DWF + 1
 
     def copy(i, k, src, dst, dev):
         return pltpu.make_async_remote_copy(src, dst, ssem.at[i], rsem.at[k], device_id=dev, device_id_type=MESH)
@@ -408,7 +414,6 @@
     ld_o = local(1, o_ref, o_v)
     ld_dy = [local(2 + s, dyg.at[:, pl.ds(512 * s, 512)], col_v.at[s]) for s in range(2)]
     ld_dq = local(4, dqkv_ref, dq_v)
-    ld_w = local(5, wg, w_v)
 
     ld_o.wait()
     ld_x = [None, None]
@@ -416,21 +421,29 @@
     for s in range(4):
         ld_dy[s].wait()
         dwo_v[:, 512 * s:512 * s + 512] = lax.dot_general(o_v[...], col_v[s % 2], TN, preferred_element_type=f32).astype(jnp.bfloat16)
+        if s == 1:
+            ld_w = local(5, wg, w_v)
         if s < 2:
             ld_dy.append(local(2 + s, dyg.at[:, pl.ds(512 * s + 1024, 512)], col_v.at[s]))
         else:
             ld_x[s - 2] = local(2 + s - 2, xg.at[:, pl.ds(mult(blocks[s - 2], t_loc), t_loc)], col_v.at[s - 2])
     row_to = 2 * y + x
+    near = x == y
     for k in range(2):
         src = dwo_v.at[:, pl.ds(k * h_loc, h_loc)]
         dst = dwo_out.at[pl.ds(mult(c, ow), ow)]
         mine = (y == k) & (row_to == r)
+        far = (y != k) & (x != y)
 
         @pl.when(mine)
         def _():
             pltpu.make_async_copy(src, dst, lsem.at[6]).start()
 
-        @pl.when(jnp.logical_not(mine))
+        @pl.when(far)
+        def _():
+            copy(DWF, DWF, src, relay, {'col': k}).start()
+
+        @pl.when(jnp.logical_not(mine | far))
         def _():
             copy(DWO + k, DWO + c, src, dst, {'col': k, 'row': row_to}).start()
 
@@ -462,6 +475,12 @@
     ld_w.wait()
     own_tok.wait()
     d_x_send(0)
+
+    @pl.when(near)
+    def _():
+        recv(DWF, relay)
+        copy(DWG, DWG + c, relay, dwo_out.at[pl.ds(mult(c, ow), ow)], {'row': 2 * (1 - y) + x}).start()
+
     d_w(2)
     send(DW + 0, dw_v.at[2], dw_slot(r), {'row': r_s})
     d_x(0, y, px_own)
@@ -478,25 +497,42 @@
     own_dw.wait()
     for k in range(3):
         recv(DW + k, dw_slot(others[k]))
+    src_col, src_x = r // 2, lax.rem(r, 2)
     for k in range(2):
         piece = dwo_out.at[pl.ds(k * ow, ow)]
-        mine = (r // 2 == y) & (2 * lax.rem(r, 2) + k == r)
+        mine = (src_col == y) & (2 * src_x + k == r)
+        far = (src_col != y) & (src_x != src_col)
 
         @pl.when(mine)
         def _():
             pltpu.make_async_copy(dwo_v.at[:, pl.ds(0, h_loc)], piece, lsem.at[6]).wait()
 
-        @pl.when(jnp.logical_not(mine))
+        @pl.when(far)
+        def _():
+            recv(DWG + k, piece)
+
+        @pl.when(jnp.logical_not(mine | far))
         def _():
             recv(DWO + k, piece)
     for cp in outs:
         cp.wait()
     for cp in started:
         cp.wait_send()
+    half = dwo_v.at[:, pl.ds(0, h_loc)]
     for k in range(2):
-        @pl.when(jnp.logical_not((y == k) & (row_to == r)))
-        def _():
-            copy(DWO + k, DWO + k, dwo_v.at[:, pl.ds(0, h_loc)], dwo_out.at[pl.ds(0, ow)], {'row': r_s}).wait_send()
+        far = (y != k) & (x != y)
+
+        @pl.when(jnp.logical_not(((y == k) & (row_to == r)) | far))
+        def _():
+            copy(DWO + k, DWO + k, half, relay, {'row': r_s}).wait_send()
+
+    @pl.when(jnp.logical_not(near))
+    def _():
+        copy(DWF, DWF, half, relay, {'col': 1 - y}).wait_send()
+
+    @pl.when(near)
+    def _():
+        copy(DWG, DWG, relay, relay, {'row': r_s}).wait_send()
 
 
 def scatter_all(x_all, dy_all, w_col, d_qkv, attn_out, blocks):
@@ -506,7 +542,7 @@
     ow = attn_out.shape[1]
     hid, feat = w_col.shape
     hbm = pl.BlockSpec(memory_space=pl.ANY)
-    n_sem = 4 * NJ + 5
+    n_sem = 4 * NJ + 9
     return pl.pallas_call(
         scatter_kernel,
         in_specs=[hbm] * 5,
@@ -516,7 +552,7 @@
             pltpu.VMEM((t_loc, feat), bf), pltpu.VMEM((seq, hw), bf), pltpu.VMEM((hid, feat), bf), pltpu.VMEM((seq, ow), bf),
             pltpu.VMEM((2, seq, t_loc), bf), pltpu.VMEM((4, t_loc, hw), bf), pltpu.VMEM((ow, hid), bf),
             pltpu.VMEM((t_loc, h_loc), f32), pltpu.VMEM((t_loc, h_loc), f32), pltpu.VMEM((t_loc, h_loc), f32),
-            pltpu.VMEM((t_loc, h_loc), bf),
+            pltpu.VMEM((t_loc, h_loc), bf), pltpu.VMEM((ow, h_loc), bf),
             pltpu.SemaphoreType.DMA((n_sem,)), pltpu.SemaphoreType.DMA((n_sem,)), pltpu.SemaphoreType.DMA((7,)),
         ],
         compiler_params=pltpu.CompilerParams(has_side_effects=True, vmem_limit_bytes=VMEM_LIMIT),

time: 265 us -> 238 us (0.90)
  Pallas kernels: 257 us -> 230 us
    pallas_call x1, Pallas kernels: 163 us -> 147 us  [forward_all(): pl.pallas_call(forward_kernel, in_specs=[hbm] * 5, out_specs=[hbm] * 6, o...]
    pallas_call x1, Pallas kernels: 94.1 us -> 83.3 us  [scatter_all(): pl.pallas_call(scatter_kernel, in_specs=[hbm] * 5, out_specs=[hbm] * 3, o...]
where the time goes in v2:
time: 238 us
  Pallas kernels  230 us (97%)
  local copies, waits for them, and re-layouts  7.08 us (3%)
    pallas_call x1, Pallas kernels, forward_all(): pl.pallas_call(forward_kernel, in_specs=[hbm] * 5, out_specs=[hbm] * 6, o...  147 us
    pallas_call x1, Pallas kernels, scatter_all(): pl.pallas_call(scatter_kernel, in_specs=[hbm] * 5, out_specs=[hbm] * 3, o...  83.3 us
    unnamed x5, local copies, waits for them, and re-layouts  7.08 us

profile of v2, /device:TPU:0, one launch (start us, length us, event | category | flops | bytes accessed | tf_op | source)
XLA Modules:
  0.0 237.6 jit_solution(11397031366623822812)
XLA Ops:
  0.6 146.5 %gather_attend.1 = (bf16[2048,2048]{1,0:T(8,128)(2,1)}, bf16[2048,2048]{1,0:T(8,128)(2,1)}, bf16[2048,3072]{1,0:T(8,128)(2,1)}, s32[4,4,128]{2,1,0:T(4,128)}, bf...) custom-call(bf16[512,1024]{1,0:T(8,128)(2,1)} %x_ref.1, bf16[512,3072]{1,0:T(8,128)(2,1)} %w_ref.1, ...), custom_call_target="tpu_custom_call" | custom-call | tf_op jit(solution)/shard_map/gather_attend/pallas_call | solution.py:341
  147.2 83.3 %project_scatter.1 = (bf16[512,1024]{1,0:T(8,128)(2,1)}, bf16[512,3072]{1,0:T(8,128)(2,1)}, bf16[512,1024]{1,0:T(8,128)(2,1)}) custom-call(bf16[2048,2048]{1,0:T(8,128)(2,1)} %get-tuple-element.8.xg, bf16[2048,2048]{1,0:T(8,128)(2,1)} %get-tuple-element.9.dyg, bf16[2048,3072]{1,0:T(8,128)(2,1)} %get-tuple-element.10.wg, ...), custom_call_target="tpu_custom_call" | custom-call | tf_op jit(solution)/shard_map/project_scatter/pallas_call | solution.py:546
  230.5 2.3 copy.11
  232.7 0.0 copy-start
  232.7 3.8 %copy.12 = bf16[512,3072]{1,0:T(8,128)(2,1)} copy(bf16[512,3072]{1,0:T(8,128)(2,1)} %get-tuple-element.17) | data formatting | bytes 6291456
  236.6 0.0 copy-done
  236.6 1.0 copy.13
Async XLA Ops:
  232.7 3.8 %copy-start = (bf16[512,1024]{1,0:T(8,128)(2,1)S(1)}, bf16[512,1024]{1,0:T(8,128)(2,1)}, u32[]{:S(2)}) copy-start(bf16[512,1024]{1,0:T(8,128)(2,1)} %get-tuple-element.18) | copy-start | bytes 3145732
